TPU v7x, 512 devices: a whole 4x4x16 slice. The times are simulated.
512 devices in a mesh: dp: 8 (over y, core), expert: 64 (over z, x).
Axes of the slice: x: 4, y: 4, z: 16, core: 2. Of those that a mesh axis runs over, the one named last changes fastest.
Arguments:
- tokens: bfloat16 [65536, 1920], P(('dp', 'expert')), may hold values from -10 to 10
- assignment: int32 [65536], P(('dp', 'expert')), may hold values from 0 to 63, as said below
- centroids: bfloat16 [64, 1920], P('expert'), may hold values from -0.125 to 0.125
- norm_gain: float32 [64, 1920], P('expert'), may hold values from 0.25 to 1.75
- inner_weight: bfloat16 [64, 4096, 1920], P('expert', 'dp'), may hold values from -0.125 to 0.125
- outer_weight: bfloat16 [64, 4096, 1920], P('expert', 'dp'), may hold values from -0.09375 to 0.09375
Outputs:
- layer_out: bfloat16 [65536, 1920], P(('dp', 'expert'))
Inputs may be any that keep to these rules, and one draw needn't show every extreme that they name: `assignment`: each expert is assigned exactly 128 of the tokens of the devices that share one index of dp. One device assigns at most 4 of its tokens to one expert, and every expert gets exactly 4 tokens from some device of each index of dp.
All inputs are finite; a program needn't handle non-finite values.
Results may differ from a plain program's by a relative error of at most 0.007.
Values may be sent and summed in bfloat16 or wider, within the bound.
A program may use at most 64 MiB of HBM per device.

v0:
```python
import jax
import jax.numpy as jnp
from jax import lax
from jax.sharding import PartitionSpec as P

epsilon = 1e-05


def in_one_piece(arrays, axis, split_dim, concat_dim, along):
    columns = [a.reshape(*a.shape[:along], -1) for a in arrays]
    both = jnp.concatenate(columns, axis=along)
    out, at, done = (
        lax.all_to_all(both, axis, split_axis=split_dim, concat_axis=concat_dim, tiled=True),
        0,
        [],
    )
    for a, column in zip(arrays, columns):
        slab = out[..., at : at + column.shape[along]]
        done.append(slab.reshape(*slab.shape[:along], *a.shape[along:]))
        at += column.shape[along]
    return tuple(done)


def normalize(rows_in, gain_row):
    values = rows_in.astype(jnp.float32)
    center = jnp.mean(values, axis=1, keepdims=True)
    spread = jnp.mean(jnp.square(values - center), axis=1, keepdims=True)
    return ((values - center) * lax.rsqrt(spread + epsilon) * gain_row).astype(jnp.bfloat16)


def expert_rows(normed, inner_mat, outer_mat):
    inner_act = lax.dot_general(
        normed, inner_mat, (((1,), (1,)), ((), ())), preferred_element_type=jnp.float32
    )
    hidden = jnp.maximum(inner_act, 0.0).astype(jnp.bfloat16)
    return jnp.dot(hidden, outer_mat, preferred_element_type=jnp.float32)


def body(tokens, assignment, centroids, norm_gain, inner_weight, outer_weight):
    tok_count = tokens.shape[0]
    experts = lax.axis_size("expert")
    capacity = 2 * tok_count // experts
    slot_total = experts * capacity
    expert_ids = jnp.arange(experts, dtype=jnp.int32)
    token_ids = jnp.arange(tok_count, dtype=jnp.int32)
    slot_ids = jnp.arange(slot_total, dtype=jnp.int32)
    onehot = (assignment[:, None] == expert_ids[None, :]).astype(jnp.int32)
    before = jnp.cumsum(onehot, axis=0) - onehot
    position = jnp.sum(before * onehot, axis=1)
    send_counts = jnp.sum(onehot, axis=0)
    slot_of = assignment * capacity + position
    matches = slot_of[None, :] == slot_ids[:, None]
    occupied = jnp.any(matches, axis=1)
    source_row = jnp.sum(jnp.where(matches, token_ids[None, :], 0), axis=1)
    outgoing = jnp.where(
        occupied[:, None], jnp.take(tokens, source_row, axis=0), jnp.zeros((), jnp.bfloat16)
    )
    arrived, arrived_counts = (
        lax.all_to_all(outgoing, "expert", split_axis=0, concat_axis=0, tiled=True),
        lax.all_to_all(send_counts, "expert", split_axis=0, concat_axis=0, tiled=True),
    )
    inclusive = jnp.cumsum(arrived_counts)
    offsets = inclusive - arrived_counts
    sender = jnp.sum((inclusive[None, :] <= token_ids[:, None]).astype(jnp.int32), axis=1)
    within = token_ids - offsets[sender]
    local_rows = jnp.take(arrived, sender * capacity + within, axis=0)
    inner_mat = inner_weight[0]
    outer_mat = outer_weight[0]
    partial_value = expert_rows(
        normalize(lax.all_gather(local_rows, "dp", axis=0, tiled=True), norm_gain),
        inner_mat,
        outer_mat,
    )
    expert_out = lax.psum_scatter(
        partial_value.astype(jnp.bfloat16), "dp", scatter_dimension=0, tiled=True
    )
    slot_sender = slot_ids // capacity
    slot_within = slot_ids % capacity
    slot_live = slot_within < arrived_counts[slot_sender]
    compact = jnp.where(slot_live, offsets[slot_sender] + slot_within, 0)
    returning = jnp.where(
        slot_live[:, None], jnp.take(expert_out, compact, axis=0), jnp.zeros((), jnp.bfloat16)
    )
    local_score = jnp.dot(local_rows, centroids[0], preferred_element_type=jnp.float32)
    local_gate = jax.nn.sigmoid(local_score).astype(jnp.bfloat16)
    gate_slots = jnp.where(slot_live, jnp.take(local_gate, compact), jnp.zeros((), jnp.bfloat16))
    back_rows, back_gate = in_one_piece((returning, gate_slots), "expert", 0, 0, 1)
    gate_value = jnp.take(back_gate, slot_of)
    combined = jnp.take(back_rows, slot_of, axis=0)
    mixed_out = tokens.astype(jnp.float32) + gate_value.astype(jnp.float32)[
        :, None
    ] * combined.astype(jnp.float32)
    return mixed_out.astype(jnp.bfloat16)


def solution(mesh):
    in_specs = (
        P(("dp", "expert"), None),
        P(("dp", "expert")),
        P("expert", None),
        P("expert", None),
        P("expert", "dp", None),
        P("expert", "dp", None),
    )
    out_specs = P(("dp", "expert"), None)
    return jax.shard_map(body, mesh=mesh, in_specs=in_specs, out_specs=out_specs, check_vma=False)
```

profile of v0, /device:TPU:25, one launch (start us, length us, event | category | flops | bytes accessed | tf_op | source)
XLA Modules:
  0.0 288.3 jit_solution(11351128227814640421)
XLA Ops:
  6.5 0.0 copy-start
  6.5 0.9 fusion.26
  7.4 0.2 reduce_window_sum.18
  7.6 0.8 fusion.27
  8.4 0.7 copy.16
  9.1 18.3 %all-to-all-start = ((s32[64,1,1]{2,1,0:T(1,128)}), s32[64,1,1]{2,1,0:T(1,128)S(1)}, u32[]{:S(2)}, u32[]{:S(2)}) async-start(s32[64,1,1]{2,1,0:T(1,128)} %copy.16), calls=%async_computation | async-start | bytes 65536 | tf_op jit(solution)/shard_map/all_to_all | solution.py:60
  27.4 0.7 compare_select_fusion.8
  28.1 0.1 select_reduce_fusion
  28.2 0.1 fusion.25
  28.4 3.4 %gather_fusion.5 = bf16[256,1920]{1,0:T(8,128)(2,1)S(1)} fusion(bf16[128,1920]{1,0:T(8,128)(2,1)} %param.10, s32[1024]{0:T(1024)S(1)} %pad_clamp_fusion.4), kind=kCustom, calls=%fused_computation.clone | custom fusion | bytes 1967104 | tf_op jit(solution)/shard_map/jit(_take)/gather | solution.py:56
  31.8 1.2 select_select_fusion.1
  33.1 2.6 all_to_all.25
  35.6 5.2 %all-to-all-done = s32[64,1,1]{2,1,0:T(1,128)S(1)} async-done(((s32[64,1,1]{2,1,0:T(1,128)}), s32[64,1,1]{2,1,0:T(1,128)S(1)}, u32[]{:S(2)}, u32[]{:S(2)}) %all-to-all-start) | async-done | bytes 288 | tf_op jit(solution)/shard_map/all_to_all | solution.py:60
  40.8 9.6 %all-to-all-start.1 = ((bf16[64,4,1920]{2,1,0:T(4,128)(2,1)}), bf16[64,4,1920]{2,1,0:T(4,128)(2,1)}, u32[]{:S(2)}, u32[]{:S(2)}) async-start(bf16[64,4,1920]{2,1,0:T(4,128)(2,1)} %all_to_all.25), calls=%async_computation.1 | async-start | bytes 1966080 | tf_op jit(solution)/shard_map/all_to_all | solution.py:59
  50.4 0.0 all-gather.2.cloned.1.call-start
  50.5 0.1 reduce-window.8
  50.6 0.1 reduce.1
  50.7 1.2 reduce
  51.9 0.1 convert_reduce_fusion.1
  52.0 1.2 gather_fusion.1
  53.3 0.0 copy-start.4
  53.3 45.7 %all-to-all-done.1 = bf16[64,4,1920]{2,1,0:T(4,128)(2,1)} async-done(((bf16[64,4,1920]{2,1,0:T(4,128)(2,1)}), bf16[64,4,1920]{2,1,0:T(4,128)(2,1)}, u32[]{:S(2)}, u32[]{:S(2)}) %all-to-all-start.1) | async-done | bytes 983072 | tf_op jit(solution)/shard_map/all_to_all | solution.py:59
  99.0 1.7 all_to_all.27
  100.7 0.9 gather_fusion.6
  101.6 0.9 broadcast_select_fusion
  102.6 0.0 all-gather.2.cloned.1.call-update
  102.6 0.2 reduce-scatter.2.cloned.1.call-start
  102.8 0.0 copy-done.4
  102.8 32.6 %all-gather.2.cloned.1.call-done = bf16[1024,1920]{1,0:T(8,128)(2,1)} async-done(((bf16[128,1920]{1,0:T(8,128)(2,1)}), bf16[1024,1920]{1,0:T(8,128)(2,1)}) %all-gather.2.cloned.1.call-update) | async-done | bytes 3932176 | tf_op jit(solution)/shard_map/all_gather | solution.py:70
  135.4 0.0 copy-start.2
  135.4 2.8 convert_reduce_fusion
  138.3 0.4 copy-done.2
  138.7 1.2 fusion.2
  139.9 0.0 copy-done
  139.9 9.2 %convolution_convert_fusion = bf16[1024,1920]{1,0:T(8,128)(2,1)} fusion(bf16[1,512,1920]{2,1,0:T(8,128)(2,1)S(1)} %copy-done, bf16[1,512,1920]{2,1,0:T(8,128)(2,1)} %param.14, bf16[1024,1920]{1,0:T(8,128)(2,1)} %all-gather.2.cloned.1.call-done, f32[1920]{0:T(1024)S(1)} %reduce.2, f32[1024]{0:T(1024)S(1)} %add_rsqrt_fusion, f32[1024]{0:T(1024)S(1)} %broadcast_multiply_fusion), kind=kOutput, calls=%fused_computation.20 | convolution fusion | flops 4039376896 | bytes 11812352 | tf_op jit(solution)/shard_map/dot_general | solution.py:36
  149.0 0.0 copy-start.3
  149.1 0.0 copy-start.5
  149.1 0.0 reduce-scatter.2.cloned.1.call-update
  149.1 1.9 gather_fusion
  151.0 1.9 gather_fusion.2
  152.9 0.1 gather.37
  153.0 0.1 gather.36
  153.1 0.0 copy-done.3
  153.1 0.0 copy-done.5
  153.2 0.2 fusion.20
  153.4 1.9 gather_fusion.3
  155.3 0.1 gather.41
  155.5 0.5 copy.18
  156.0 39.2 %reduce-scatter.2.cloned.1.call-done = bf16[128,1920]{1,0:T(8,128)(2,1)} async-done(((bf16[1024,1920]{1,0:T(8,128)(2,1)}), bf16[128,1920]{1,0:T(8,128)(2,1)}) %reduce-scatter.2.cloned.1.call-update) | async-done | bytes 491536 | tf_op jit(solution)/shard_map/reduce_scatter | solution.py:74
  195.1 3.4 %gather_fusion.7 = bf16[256,1920]{1,0:T(8,128)(2,1)S(1)} fusion(bf16[128,1920]{1,0:T(8,128)(2,1)} %reduce-scatter.2.cloned.1.call-done, s32[1024]{0:T(1024)S(1)} %pad_clamp_fusion.2), kind=kCustom, calls=%fused_computation.2.clone | custom fusion | bytes 1967104 | tf_op jit(solution)/shard_map/jit(_take)/gather | solution.py:82
  198.6 1.2 select_select_fusion
  199.8 1.8 concatenate.6
  201.6 1.6 pad_maximum_fusion
  203.3 14.3 %all-to-all-start.2 = ((bf16[64,4,1921]{2,1,0:T(4,128)(2,1)}), bf16[64,4,1921]{2,1,0:T(4,128)(2,1)S(1)}, u32[]{:S(2)}, u32[]{:S(2)}) async-start(bf16[64,4,1921]{2,1,0:T(4,128)(2,1)} %pad_maximum_fusion), calls=%async_computation.3 | async-start | bytes 2097152 | tf_op jit(solution)/shard_map/all_to_all | solution.py:13
  217.6 55.2 %all-to-all-done.2 = bf16[64,4,1921]{2,1,0:T(4,128)(2,1)S(1)} async-done(((bf16[64,4,1921]{2,1,0:T(4,128)(2,1)}), bf16[64,4,1921]{2,1,0:T(4,128)(2,1)S(1)}, u32[]{:S(2)}, u32[]{:S(2)}) %all-to-all-start.2) | async-done | bytes 983584 | tf_op jit(solution)/shard_map/all_to_all | solution.py:13
  272.8 1.3 all_to_all.29
  274.1 0.0 copy-start.1
  274.1 1.3 slice.27
  275.4 0.9 slice_reduce_fusion
  276.4 1.7 gather_fusion.8
  278.1 1.2 gather_fusion.4
  279.3 0.0 copy-done.1
  279.3 2.1 add_convert_fusion
  (20 shorter events, 0.2 us)
Async XLA Ops:
  6.5 133.3 %copy-start = (bf16[1,512,1920]{2,1,0:T(8,128)(2,1)S(1)}, bf16[1,512,1920]{2,1,0:T(8,128)(2,1)}, u32[]{:S(2)}) copy-start(bf16[1,512,1920]{2,1,0:T(8,128)(2,1)} %param.15) | copy-start | bytes 5898244
  9.1 31.7 %all-to-all-start = ((s32[64,1,1]{2,1,0:T(1,128)}), s32[64,1,1]{2,1,0:T(1,128)S(1)}, u32[]{:S(2)}, u32[]{:S(2)}) async-start(s32[64,1,1]{2,1,0:T(1,128)} %copy.16), calls=%async_computation | async-start | bytes 65536 | tf_op jit(solution)/shard_map/all_to_all | solution.py:60
  40.8 58.2 %all-to-all-start.1 = ((bf16[64,4,1920]{2,1,0:T(4,128)(2,1)}), bf16[64,4,1920]{2,1,0:T(4,128)(2,1)}, u32[]{:S(2)}, u32[]{:S(2)}) async-start(bf16[64,4,1920]{2,1,0:T(4,128)(2,1)} %all_to_all.25), calls=%async_computation.1 | async-start | bytes 1966080 | tf_op jit(solution)/shard_map/all_to_all | solution.py:59
  50.4 85.0 %all-gather.2.cloned.1.call-start = ((), (), s32[]{:S(2)}) async-start(), calls=%async_computation.4 | async-start | bytes 4423680 | tf_op jit(solution)/shard_map/all_gather | solution.py:70
  53.3 49.5 %copy-start.4 = (f32[1,1920]{1,0:T(1,128)S(1)}, f32[1,1920]{1,0:T(1,128)}, u32[]{:S(2)}) copy-start(f32[1,1920]{1,0:T(1,128)} %param.13) | copy-start | bytes 23044
  102.6 92.6 %reduce-scatter.2.cloned.1.call-start = ((), (), s32[]{:S(2)}) async-start(), calls=%async_computation.5 | async-start | bytes 4423680 | tf_op jit(solution)/shard_map/reduce_scatter | solution.py:74
  135.4 3.3 %copy-start.2 = (bf16[1024,1920]{1,0:T(8,128)(2,1)S(1)}, bf16[1024,1920]{1,0:T(8,128)(2,1)}, u32[]{:S(2)}) copy-start(bf16[1024,1920]{1,0:T(8,128)(2,1)} %all-gather.2.cloned.1.call-done) | copy-start | bytes 11796484
  149.0 4.1 %copy-start.3 = (bf16[128,1920]{1,0:T(8,128)(2,1)S(1)}, bf16[128,1920]{1,0:T(8,128)(2,1)}, u32[]{:S(2)}) copy-start(bf16[128,1920]{1,0:T(8,128)(2,1)} %broadcast_select_fusion) | copy-start | bytes 1474564
  149.1 4.1 %copy-start.5 = (bf16[1,1920]{1,0:T(2,128)(2,1)S(1)}, bf16[1,1920]{1,0:T(2,128)(2,1)}, u32[]{:S(2)}) copy-start(bf16[1,1920]{1,0:T(2,128)(2,1)} %param.12) | copy-start | bytes 11524
  203.3 69.5 %all-to-all-start.2 = ((bf16[64,4,1921]{2,1,0:T(4,128)(2,1)}), bf16[64,4,1921]{2,1,0:T(4,128)(2,1)S(1)}, u32[]{:S(2)}, u32[]{:S(2)}) async-start(bf16[64,4,1921]{2,1,0:T(4,128)(2,1)} %pad_maximum_fusion), calls=%async_computation.3 | async-start | bytes 2097152 | tf_op jit(solution)/shard_map/all_to_all | solution.py:13
  274.1 5.3 %copy-start.1 = (bf16[128,1920]{1,0:T(8,128)(2,1)S(1)}, bf16[128,1920]{1,0:T(8,128)(2,1)}, u32[]{:S(2)}) copy-start(bf16[128,1920]{1,0:T(8,128)(2,1)} %param.10) | copy-start | bytes 1474564
Sparse Core Ops, SparseCore 0:
  102.7 32.6 all-gather.1
  149.2 45.8 reduce-scatter.1
where the time goes:
time: 289 us; the launch traced here: 288 us
  waiting for transfers between devices  178 us (62%)
  starting transfers between devices  42.5 us (15%)
  local copies, waits for them, and re-layouts  29.3 us (10%)
  other arithmetic  15.6 us (5%)
  between operations  13.7 us (5%)
  matrix products  9.41 us (3%)
    all_to_all x1, waiting for transfers between devices, in_one_piece(): lax.all_to_all(both, axis, split_axis=split_dim, concat_axis=concat_dim,...  55.2 us
    all_to_all x1, waiting for transfers between devices, body(): lax.all_to_all(outgoing, 'expert', split_axis=0, concat_axis=0, tiled=True)  45.7 us
    reduce_scatter x1, waiting for transfers between devices, body(): lax.psum_scatter(partial_value.astype(jnp.bfloat16), 'dp', scatter_dimens...  39.2 us
    all_gather x1, waiting for transfers between devices, body(): lax.all_gather(local_rows, 'dp', axis=0, tiled=True)  32.6 us
    all_to_all x1, starting transfers between devices, body(): lax.all_to_all(send_counts, 'expert', split_axis=0, concat_axis=0, tiled=...  18.3 us
    all_to_all x1, starting transfers between devices, in_one_piece(): lax.all_to_all(both, axis, split_axis=split_dim, concat_axis=concat_dim,...  14.3 us
    all_to_all x1, starting transfers between devices, body(): lax.all_to_all(outgoing, 'expert', split_axis=0, concat_axis=0, tiled=True)  9.56 us
    dot_general x1, matrix products, expert_rows(): return jnp.dot(hidden, outer_mat, preferred_element_type=jnp.float32)  9.17 us
  transfers between devices with their start and end apart: 5, of which 5 were waited for; matrix products, arithmetic and copies ran while one was open for 5% of the time, Pallas kernels for 0%

commit v1 on v0

--- a/solution.py
+++ b/solution.py
@@ -4,6 +4,14 @@
 from jax.sharding import PartitionSpec as P
 
 epsilon = 1e-05
+
+
+def tiled_gather(array, axis, dim):
+    devices = lax.axis_size(axis)
+    repeats = [devices if d == dim else 1 for d in range(array.ndim)]
+    return lax.all_to_all(
+        jnp.tile(array, repeats), axis, split_axis=dim, concat_axis=dim, tiled=True
+    )
 
 
 def in_one_piece(arrays, axis, split_dim, concat_dim, along):
@@ -67,9 +75,7 @@
     inner_mat = inner_weight[0]
     outer_mat = outer_weight[0]
     partial_value = expert_rows(
-        normalize(lax.all_gather(local_rows, "dp", axis=0, tiled=True), norm_gain),
-        inner_mat,
-        outer_mat,
+        normalize(tiled_gather(local_rows, "dp", 0), norm_gain), inner_mat, outer_mat
     )
     expert_out = lax.psum_scatter(
         partial_value.astype(jnp.bfloat16), "dp", scatter_dimension=0, tiled=True

time: 289 us -> 307 us (1.062)
  starting transfers between devices: 42.5 us -> 51.4 us
  other arithmetic: 15.6 us -> 21 us
    all_to_all x0 -> x1, waiting for transfers between devices: none -> 44.3 us  [tiled_gather(): lax.all_to_all(jnp.tile(array, repeats), axis, split_axis=dim, concat_axi...]
    all_gather x1 -> x0, waiting for transfers between devices: 32.6 us -> none  [body(): lax.all_gather(local_rows, 'dp', axis=0, tiled=True)]
    reduce_scatter x1, waiting for transfers between devices: 39.2 us -> 29.3 us  [body(): lax.psum_scatter(partial_value.astype(jnp.bfloat16), 'dp', scatter_dimens...]
    all_to_all x0 -> x1, starting transfers between devices: none -> 9.15 us  [tiled_gather(): lax.all_to_all(jnp.tile(array, repeats), axis, split_axis=dim, concat_axi...]
    convert_element_type x0 -> x1, other arithmetic: none -> 4.17 us  [normalize(): ((values - center) * lax.rsqrt(spread + epsilon) * gain_row).astype(jnp.b...]
where the time goes in v1:
time: 307 us; the launch traced here: 306 us
  waiting for transfers between devices  180 us (59%)
  starting transfers between devices  51.4 us (17%)
  local copies, waits for them, and re-layouts  31.3 us (10%)
  other arithmetic  21 us (7%)
  between operations  13.7 us (4%)
  matrix products  9.38 us (3%)
    all_to_all x1, waiting for transfers between devices, in_one_piece(): lax.all_to_all(both, axis, split_axis=split_dim, concat_axis=concat_dim,...  55.2 us
    all_to_all x1, waiting for transfers between devices, body(): lax.all_to_all(outgoing, 'expert', split_axis=0, concat_axis=0, tiled=True)  45.8 us
    all_to_all x1, waiting for transfers between devices, tiled_gather(): lax.all_to_all(jnp.tile(array, repeats), axis, split_axis=dim, concat_axi...  44.3 us
    reduce_scatter x1, waiting for transfers between devices, body(): lax.psum_scatter(partial_value.astype(jnp.bfloat16), 'dp', scatter_dimens...  29.3 us
    all_to_all x1, starting transfers between devices, body(): lax.all_to_all(send_counts, 'expert', split_axis=0, concat_axis=0, tiled=...  18.3 us
    all_to_all x1, starting transfers between devices, in_one_piece(): lax.all_to_all(both, axis, split_axis=split_dim, concat_axis=concat_dim,...  14.4 us
    all_to_all x1, starting transfers between devices, body(): lax.all_to_all(outgoing, 'expert', split_axis=0, concat_axis=0, tiled=True)  9.56 us
    all_to_all x1, starting transfers between devices, tiled_gather(): lax.all_to_all(jnp.tile(array, repeats), axis, split_axis=dim, concat_axi...  9.15 us
  transfers between devices with their start and end apart: 5, of which 5 were waited for; matrix products, arithmetic and copies ran while one was open for 5% of the time, Pallas kernels for 0%

profile of v1, /device:TPU:25, one launch (start us, length us, event | category | flops | bytes accessed | tf_op | source)
XLA Modules:
  0.0 306.4 jit_solution(12103659754098635736)
XLA Ops:
  6.5 0.0 copy-start
  6.5 0.9 fusion.18
  7.4 0.2 reduce_window_sum.18
  7.6 0.8 fusion.19
  8.4 0.7 copy.16
  9.1 18.3 %all-to-all-start = ((s32[64,1,1]{2,1,0:T(1,128)}), s32[64,1,1]{2,1,0:T(1,128)S(1)}, u32[]{:S(2)}, u32[]{:S(2)}) async-start(s32[64,1,1]{2,1,0:T(1,128)} %copy.16), calls=%async_computation | async-start | bytes 65536 | tf_op jit(solution)/shard_map/all_to_all | solution.py:68
  27.4 0.7 compare_select_fusion.8
  28.1 0.1 select_reduce_fusion
  28.2 0.1 fusion.17
  28.4 3.4 %gather_fusion.5 = bf16[256,1920]{1,0:T(8,128)(2,1)S(1)} fusion(bf16[128,1920]{1,0:T(8,128)(2,1)} %param.10, s32[1024]{0:T(1024)S(1)} %pad_clamp_fusion.4), kind=kCustom, calls=%fused_computation.clone | custom fusion | bytes 1967104 | tf_op jit(solution)/shard_map/jit(_take)/gather | solution.py:64
  31.8 1.2 select_select_fusion.1
  33.1 2.6 all_to_all.29
  35.6 5.2 %all-to-all-done = s32[64,1,1]{2,1,0:T(1,128)S(1)} async-done(((s32[64,1,1]{2,1,0:T(1,128)}), s32[64,1,1]{2,1,0:T(1,128)S(1)}, u32[]{:S(2)}, u32[]{:S(2)}) %all-to-all-start) | async-done | bytes 288 | tf_op jit(solution)/shard_map/all_to_all | solution.py:68
  40.8 9.6 %all-to-all-start.1 = ((bf16[64,4,1920]{2,1,0:T(4,128)(2,1)}), bf16[64,4,1920]{2,1,0:T(4,128)(2,1)}, u32[]{:S(2)}, u32[]{:S(2)}) async-start(bf16[64,4,1920]{2,1,0:T(4,128)(2,1)} %all_to_all.29), calls=%async_computation.1 | async-start | bytes 1966080 | tf_op jit(solution)/shard_map/all_to_all | solution.py:67
  50.4 0.1 reduce-window.8
  50.5 0.1 reduce.3
  50.6 1.2 reduce.2
  51.9 0.1 convert_reduce_fusion.1
  52.0 1.2 gather_fusion.1
  53.2 45.8 %all-to-all-done.1 = bf16[64,4,1920]{2,1,0:T(4,128)(2,1)} async-done(((bf16[64,4,1920]{2,1,0:T(4,128)(2,1)}), bf16[64,4,1920]{2,1,0:T(4,128)(2,1)}, u32[]{:S(2)}, u32[]{:S(2)}) %all-to-all-start.1) | async-done | bytes 983072 | tf_op jit(solution)/shard_map/all_to_all | solution.py:67
  99.0 1.7 all_to_all.31
  100.7 0.9 gather_fusion.6
  101.6 0.1 broadcast_select_fusion
  101.8 2.4 tile.2
  104.2 0.0 copy-start.2
  104.2 9.1 %all-to-all-start.2 = ((bf16[8,128,1920]{2,1,0:T(8,128)(2,1)}), bf16[8,128,1920]{2,1,0:T(8,128)(2,1)}, u32[]{:S(2)}, u32[]{:S(2)}) async-start(bf16[8,128,1920]{2,1,0:T(8,128)(2,1)} %tile.2), calls=%async_computation.2 | async-start | bytes 7864320 | tf_op jit(solution)/shard_map/all_to_all | solution.py:12
  113.3 0.0 reduce-scatter.2.cloned.1.call-start
  113.3 0.0 copy-done.2
  113.4 44.3 %all-to-all-done.2 = bf16[8,128,1920]{2,1,0:T(8,128)(2,1)} async-done(((bf16[8,128,1920]{2,1,0:T(8,128)(2,1)}), bf16[8,128,1920]{2,1,0:T(8,128)(2,1)}, u32[]{:S(2)}, u32[]{:S(2)}) %all-to-all-start.2) | async-done | bytes 3932192 | tf_op jit(solution)/shard_map/all_to_all | solution.py:12
  157.6 2.7 convert_reduce_fusion
  160.3 3.3 %fusion.2 = f32[8,128]{1,0:T(8,128)S(1)} fusion(bf16[8,128,1920]{2,1,0:T(8,128)(2,1)} %all-to-all-done.2, f32[8,128]{1,0:T(8,128)S(1)} %broadcast_multiply_fusion), kind=kLoop, calls=%fused_computation.13 | loop fusion | flops 7863296 | bytes 3940352 | tf_op jit(solution)/shard_map/reduce_sum | solution.py:35
  163.6 4.2 %fusion.4 = bf16[8,128,1920]{2,1,0:T(8,128)(2,1)} fusion(bf16[8,128,1920]{2,1,0:T(8,128)(2,1)} %all-to-all-done.2, f32[1920]{0:T(1024)S(1)} %reduce.4, f32[8,128]{1,0:T(8,128)S(1)} %add_rsqrt_fusion, f32[8,128]{1,0:T(8,128)S(1)} %broadcast_multiply_fusion), kind=kLoop, calls=%fused_computation.15 | loop fusion | flops 9830400 | bytes 7880192 | tf_op jit(solution)/shard_map/convert_element_type | solution.py:36
  167.8 0.0 copy-done
  167.8 9.1 %convolution_convert_fusion = bf16[1024,1920]{1,0:T(8,128)(2,1)} fusion(bf16[1,512,1920]{2,1,0:T(8,128)(2,1)S(1)} %copy-done, bf16[1024,1920]{1,0:T(8,128)(2,1)} %bitcast.38, bf16[1,512,1920]{2,1,0:T(8,128)(2,1)} %param.14), kind=kOutput, calls=%fused_computation.16 | convolution fusion | flops 4029546496 | bytes 11796480 | tf_op jit(solution)/shard_map/dot_general | solution.py:44
  176.9 0.0 copy-start.3
  177.0 0.0 reduce-scatter.2.cloned.1.call-update
  177.0 1.9 gather_fusion
  178.9 1.9 gather_fusion.2
  180.8 0.1 gather.37
  180.9 0.1 gather.36
  181.0 0.0 copy-done.3
  181.0 0.2 fusion.14
  181.3 1.9 gather_fusion.3
  183.2 0.1 gather.41
  183.4 0.5 copy.18
  183.9 29.3 %reduce-scatter.2.cloned.1.call-done = bf16[128,1920]{1,0:T(8,128)(2,1)} async-done(((bf16[1024,1920]{1,0:T(8,128)(2,1)}), bf16[128,1920]{1,0:T(8,128)(2,1)}) %reduce-scatter.2.cloned.1.call-update) | async-done | bytes 491536 | tf_op jit(solution)/shard_map/reduce_scatter | solution.py:80
  213.1 3.4 %gather_fusion.7 = bf16[256,1920]{1,0:T(8,128)(2,1)S(1)} fusion(bf16[128,1920]{1,0:T(8,128)(2,1)} %reduce-scatter.2.cloned.1.call-done, s32[1024]{0:T(1024)S(1)} %pad_clamp_fusion.2), kind=kCustom, calls=%fused_computation.2.clone | custom fusion | bytes 1967104 | tf_op jit(solution)/shard_map/jit(_take)/gather | solution.py:88
  216.6 1.2 select_select_fusion
  217.8 1.8 concatenate.6
  219.6 1.6 pad_maximum_fusion
  221.3 14.4 %all-to-all-start.3 = ((bf16[64,4,1921]{2,1,0:T(4,128)(2,1)}), bf16[64,4,1921]{2,1,0:T(4,128)(2,1)S(1)}, u32[]{:S(2)}, u32[]{:S(2)}) async-start(bf16[64,4,1921]{2,1,0:T(4,128)(2,1)} %pad_maximum_fusion), calls=%async_computation.4 | async-start | bytes 2097152 | tf_op jit(solution)/shard_map/all_to_all | solution.py:21
  235.7 55.2 %all-to-all-done.3 = bf16[64,4,1921]{2,1,0:T(4,128)(2,1)S(1)} async-done(((bf16[64,4,1921]{2,1,0:T(4,128)(2,1)}), bf16[64,4,1921]{2,1,0:T(4,128)(2,1)S(1)}, u32[]{:S(2)}, u32[]{:S(2)}) %all-to-all-start.3) | async-done | bytes 983584 | tf_op jit(solution)/shard_map/all_to_all | solution.py:21
  290.8 1.3 all_to_all.34
  292.1 0.0 copy-start.1
  292.1 1.3 slice.27
  293.5 0.9 slice_reduce_fusion
  294.4 1.7 gather_fusion.8
  296.1 1.2 gather_fusion.4
  297.4 0.0 copy-done.1
  297.4 2.1 add_convert_fusion
  (20 shorter events, 0.2 us)
Async XLA Ops:
  6.5 161.3 %copy-start = (bf16[1,512,1920]{2,1,0:T(8,128)(2,1)S(1)}, bf16[1,512,1920]{2,1,0:T(8,128)(2,1)}, u32[]{:S(2)}) copy-start(bf16[1,512,1920]{2,1,0:T(8,128)(2,1)} %param.15) | copy-start | bytes 5898244
  9.1 31.7 %all-to-all-start = ((s32[64,1,1]{2,1,0:T(1,128)}), s32[64,1,1]{2,1,0:T(1,128)S(1)}, u32[]{:S(2)}, u32[]{:S(2)}) async-start(s32[64,1,1]{2,1,0:T(1,128)} %copy.16), calls=%async_computation | async-start | bytes 65536 | tf_op jit(solution)/shard_map/all_to_all | solution.py:68
  40.8 58.2 %all-to-all-start.1 = ((bf16[64,4,1920]{2,1,0:T(4,128)(2,1)}), bf16[64,4,1920]{2,1,0:T(4,128)(2,1)}, u32[]{:S(2)}, u32[]{:S(2)}) async-start(bf16[64,4,1920]{2,1,0:T(4,128)(2,1)} %all_to_all.29), calls=%async_computation.1 | async-start | bytes 1966080 | tf_op jit(solution)/shard_map/all_to_all | solution.py:67
  104.2 9.2 %copy-start.2 = (f32[1,1920]{1,0:T(1,128)S(1)}, f32[1,1920]{1,0:T(1,128)}, u32[]{:S(2)}) copy-start(f32[1,1920]{1,0:T(1,128)} %param.13) | copy-start | bytes 23044
  104.2 53.4 %all-to-all-start.2 = ((bf16[8,128,1920]{2,1,0:T(8,128)(2,1)}), bf16[8,128,1920]{2,1,0:T(8,128)(2,1)}, u32[]{:S(2)}, u32[]{:S(2)}) async-start(bf16[8,128,1920]{2,1,0:T(8,128)(2,1)} %tile.2), calls=%async_computation.2 | async-start | bytes 7864320 | tf_op jit(solution)/shard_map/all_to_all | solution.py:12
  113.3 99.8 %reduce-scatter.2.cloned.1.call-start = ((), (), s32[]{:S(2)}) async-start(), calls=%async_computation.5 | async-start | bytes 4423680 | tf_op jit(solution)/shard_map/reduce_scatter | solution.py:80
  176.9 4.1 %copy-start.3 = (bf16[1,1920]{1,0:T(2,128)(2,1)S(1)}, bf16[1,1920]{1,0:T(2,128)(2,1)}, u32[]{:S(2)}) copy-start(bf16[1,1920]{1,0:T(2,128)(2,1)} %param.12) | copy-start | bytes 11524
  221.3 69.6 %all-to-all-start.3 = ((bf16[64,4,1921]{2,1,0:T(4,128)(2,1)}), bf16[64,4,1921]{2,1,0:T(4,128)(2,1)S(1)}, u32[]{:S(2)}, u32[]{:S(2)}) async-start(bf16[64,4,1921]{2,1,0:T(4,128)(2,1)} %pad_maximum_fusion), calls=%async_computation.4 | async-start | bytes 2097152 | tf_op jit(solution)/shard_map/all_to_all | solution.py:21
  292.1 5.3 %copy-start.1 = (bf16[128,1920]{1,0:T(8,128)(2,1)S(1)}, bf16[128,1920]{1,0:T(8,128)(2,1)}, u32[]{:S(2)}) copy-start(bf16[128,1920]{1,0:T(8,128)(2,1)} %param.10) | copy-start | bytes 1474564
Sparse Core Ops, SparseCore 0:
  177.1 36.0 reduce-scatter.1
